TPU v7x, 32 devices: a whole 2x2x4 slice. The times are simulated.
32 devices in a mesh: dp: 4 (over z), row: 2 (over y), col: 4 (over x, core).
Axes of the slice: x: 2, y: 2, z: 4, core: 2. Of those that a mesh axis runs over, the one named last changes fastest.
Arguments:
- activations: bfloat16 [4096, 4096], P('dp', 'col'), may hold values from -6 to 6
- out_grad: bfloat16 [4096, 14336], P('dp', 'row'), may hold values from -6 to 6
- weight: float32 [2, 7168, 4096], P('row', 'dp', 'col'), as said below
- step_size: float32 [2, 7168], P('row'), may hold values from 0.001 to 0.016
Outputs:
- input_grad: bfloat16 [4096, 4096], P(('dp', 'row'), 'col')
- weight_grad: float32 [2, 7168, 4096], P('row', 'dp', 'col')
- step_grad: float32 [2, 7168], P('row', 'dp')
Inputs may be any that keep to these rules, and one draw needn't show every extreme that they name: Each latent weight divided by its row's step lies at least 0.1 away from every multiple of one half.
All inputs are finite; a program needn't handle non-finite values.
Results may differ from a plain program's by a relative error of at most 0.0096.
Values may be sent and summed in bfloat16 or wider, within the bound.
A program may use at most 128 MiB of HBM per device.

v0:
```python
import jax
import jax.numpy as jnp
from jax import lax
from jax.sharding import PartitionSpec as P

D = 4096


def quantize(latent, scales):
    ratio = latent / scales[:, None]
    clipped = jnp.clip(ratio, -8.0, 7.0)
    levels = jnp.floor(clipped + 0.5)
    inside = jnp.where((ratio >= -8.0) & (ratio <= 7.0), 1.0, 0.0).astype(jnp.float32)
    factor = jnp.where(inside > 0.5, levels - ratio, clipped)
    quantized = (levels * scales[:, None]).astype(jnp.bfloat16)
    return (quantized, inside, factor)


def shift(block, axis, count, by):
    return lax.ppermute(block, axis, [(i, (i + by) % count) for i in range(count)])


def swap(block, axis, count, bit):
    return lax.ppermute(block, axis, [(i, i ^ bit) for i in range(count)])


def gather_rows(block, axis, count):
    position = lax.axis_index(axis)
    bit = 1
    bits = []
    while bit < count:
        bits.append(bit)
        bit *= 2
    pieces = {0: block}
    for bit in reversed(bits):
        held = dict(pieces)
        for key in held:
            pieces[key ^ bit] = swap(held[key], axis, count, bit)
    parts = [pieces[key] for key in range(count)]
    for bit in bits:
        flag = position & bit != 0
        parts = [jnp.where(flag, parts[key ^ bit], parts[key]) for key in range(count)]
    return jnp.concatenate(parts, axis=0)


def make_shards(n_dp, n_row, n_col):

    def shards(activations, out_grad, weight, step_size):
        own_count = weight.shape[1]
        tokens = out_grad.shape[0]
        dp = lax.axis_index("dp")
        row = lax.axis_index("row")
        col = lax.axis_index("col")
        scales = step_size[0]
        own_scales = lax.dynamic_slice_in_dim(scales, dp * own_count, own_count, 0)
        grad_factor = 1.0 / (7.0 * D) ** 0.5
        share = tokens // n_col
        half = tokens // n_row
        mine = lax.dynamic_slice_in_dim(out_grad, col * share, share, 0)
        ring = lax.dynamic_slice_in_dim(activations, row * half, half, 0)
        grads, acts = ([], [])
        for k in range(1, n_dp):
            target = (dp + k) % n_dp
            chunk = lax.dynamic_slice_in_dim(mine, target * own_count, own_count, 1)
            grads.append(shift(chunk, "dp", n_dp, k))
            ring = shift(ring, "dp", n_dp, 1)
            acts.append(ring)
        quantized, inside, factor = quantize(weight[0], own_scales)
        own_grad = lax.dynamic_slice_in_dim(out_grad, dp * own_count, own_count, 1)

        def reduced(grad):
            size = tokens
            bit = n_row // 2
            if bit == 0:
                return jnp.dot(grad, quantized, preferred_element_type=jnp.float32)
            size //= 2
            upper = (row // bit % 2).astype(jnp.int32)
            sent = lax.dynamic_slice_in_dim(grad, (1 - upper) * size, size, 0)
            kept = lax.dynamic_slice_in_dim(grad, upper * size, size, 0)
            out = jnp.dot(sent, quantized, preferred_element_type=jnp.float32).astype(jnp.bfloat16)
            came = swap(out, "row", n_row, bit)
            total = jnp.dot(kept, quantized, preferred_element_type=jnp.float32) + came.astype(
                jnp.float32
            )
            bit //= 2
            while bit:
                size //= 2
                upper = row // bit % 2 == 1
                low, high = (total[:size], total[size:])
                came = swap(jnp.where(upper, low, high).astype(jnp.bfloat16), "row", n_row, bit)
                total = jnp.where(upper, high, low) + came.astype(jnp.float32)
                bit //= 2
            return total

        products = lax.dot_general(
            own_grad, activations, (((0,), (0,)), ((), ())), preferred_element_type=jnp.float32
        )
        own_total = reduced(own_grad)
        running = None
        for k in range(1, n_dp):
            grad = gather_rows(grads[k - 1], "col", n_col)
            total = reduced(grad)
            if running is not None:
                total = total + running.astype(jnp.float32)
            running = shift(total.astype(jnp.bfloat16), "dp", n_dp, 1)
            act = gather_rows(acts[k - 1], "row", n_row)
            products = products + lax.dot_general(
                grad, act, (((0,), (0,)), ((), ())), preferred_element_type=jnp.float32
            )
        if running is not None:
            own_total = own_total + running.astype(jnp.float32)
        input_grad = own_total.astype(jnp.bfloat16)
        step_rows = lax.psum(jnp.sum(products * factor, axis=1) * grad_factor, "col")
        weight_grad = (products * inside)[None]
        return (input_grad, weight_grad, step_rows[None])

    return shards


def solution(mesh):
    in_specs = (P("dp", "col"), P("dp", "row"), P("row", "dp", "col"), P("row", None))
    out_specs = (P(("dp", "row"), "col"), P("row", "dp", "col"), P("row", "dp"))
    shards = make_shards(mesh.shape["dp"], mesh.shape["row"], mesh.shape["col"])
    return jax.shard_map(shards, mesh=mesh, in_specs=in_specs, out_specs=out_specs, check_vma=False)
```

profile of v0, /device:TPU:0, one launch (start us, length us, event | category | flops | bytes accessed | tf_op | source)
XLA Modules:
  0.0 330.7 jit_solution(6011322174611351139)
XLA Ops:
  6.3 4.7 %fusion.58 = (bf16[256,1792]{1,0:T(8,128)(2,1)}, bf16[256,1792]{1,0:T(8,128)(2,1)}, bf16[256,1792]{1,0:T(8,128)(2,1)S(1)}) fusion(bf16[1024,7168]{1,0:T(8,128)(2,1)} %param.5, s32[]{:T(128)S(6)} %select_n.223, s32[]{:T(128)S(6)} %select_n.226, s32[]{:T(128)S(6)} %select_n.237, s32[]{:T(128)S(6)} %select_n.248), kind=kLoop, calls=%fused_computation.92 | loop fusion | bytes 5505040 | tf_op jit(solution)/shard_map/dynamic_slice | solution.py:64
  12.6 20.0 %collective-permute-done.19 = bf16[512,1024]{1,0:T(8,128)(2,1)S(1)} collective-permute-done((bf16[512,1024]{1,0:T(8,128)(2,1)}, bf16[512,1024]{1,0:T(8,128)(2,1)S(1)}, u32[]{:S(2)}, u32[]{:S(2)}) %collective-permute-start.19) | collective-permute-done | bytes 1048608 | tf_op jit(solution)/shard_map/ppermute | solution.py:20
  36.1 16.3 %collective-permute-done.11 = bf16[256,1792]{1,0:T(8,128)(2,1)} collective-permute-done((bf16[256,1792]{1,0:T(8,128)(2,1)S(1)}, bf16[256,1792]{1,0:T(8,128)(2,1)}, u32[]{:S(2)}, u32[]{:S(2)}) %collective-permute-start.11) | collective-permute-done | bytes 917536 | tf_op jit(solution)/shard_map/ppermute | solution.py:20
  54.1 8.4 %copy.7 = f32[1,1792,1024]{1,2,0:T(8,128)} copy(f32[1,1792,1024]{2,1,0:T(8,128)} %param.6) | data formatting | bytes 14680064 | tf_op args[2]
  63.3 7.9 %collective-permute-done.1 = bf16[256,1792]{1,0:T(8,128)(2,1)} collective-permute-done((bf16[256,1792]{1,0:T(8,128)(2,1)}, bf16[256,1792]{1,0:T(8,128)(2,1)}, u32[]{:S(2)}, u32[]{:S(2)}) %collective-permute-start.1) | collective-permute-done | bytes 917536 | tf_op jit(solution)/shard_map/ppermute | solution.py:20
  72.7 37.7 %collective-permute-done.6 = bf16[256,1792]{1,0:T(8,128)(2,1)} collective-permute-done((bf16[256,1792]{1,0:T(8,128)(2,1)}, bf16[256,1792]{1,0:T(8,128)(2,1)}, u32[]{:S(2)}, u32[]{:S(2)}) %collective-permute-start.6) | collective-permute-done | bytes 917536 | tf_op jit(solution)/shard_map/ppermute | solution.py:20
  112.0 8.2 %fusion.1 = f32[1792,1024]{0,1:T(8,128)} fusion(bf16[1024,1024]{1,0:T(8,128)(2,1)S(1)} %copy-done, bf16[1024,7168]{1,0:T(8,128)(2,1)} %param.5, s32[]{:T(128)S(6)} %select_n.216), kind=kOutput, calls=%fused_computation.12 | convolution fusion | flops 3758096384 | bytes 13107204 | tf_op jit(solution)/shard_map/dot_general | solution.py:95
  122.3 10.7 %collective-permute-done.7 = bf16[256,1792]{1,0:T(8,128)(2,1)S(1)} collective-permute-done((bf16[256,1792]{1,0:T(8,128)(2,1)}, bf16[256,1792]{1,0:T(8,128)(2,1)S(1)}, u32[]{:S(2)}, u32[]{:S(2)}) %collective-permute-start.7) | collective-permute-done | bytes 917536 | tf_op jit(solution)/shard_map/ppermute | solution.py:24
  132.9 5.6 %collective-permute-done.21 = bf16[512,1024]{1,0:T(8,128)(2,1)S(1)} collective-permute-done((bf16[512,1024]{1,0:T(8,128)(2,1)S(1)}, bf16[512,1024]{1,0:T(8,128)(2,1)S(1)}, u32[]{:S(2)}, u32[]{:S(2)}) %collective-permute-start.21) | collective-permute-done | bytes 1048608 | tf_op jit(solution)/shard_map/ppermute | solution.py:20
  141.9 6.7 %fusion.3 = f32[1792,1024]{0,1:T(8,128)} fusion(bf16[512,1024]{1,0:T(8,128)(2,1)S(1)} %get-tuple-element.27, bf16[512,1024]{1,0:T(8,128)(2,1)S(1)} %get-tuple-element.26, bf16[256,1792]{1,0:T(8,128)(2,1)S(1)} %get-tuple-element.23, bf16[256,1792]{1,0:T(8,128)(2,1)S(1)} %get-tuple-element.22, bf16[256,1792]{1,0:T(8,128)(2,1)S(1)} %get-tuple-element.21, ...), kind=kOutput, calls=%fused_computation.14 | convolution fusion | flops 3776970752 | bytes 13107200 | tf_op jit(solution)/shard_map/dot_general | solution.py:107
  148.6 6.0 %collective-permute-start.23 = (bf16[512,1024]{1,0:T(8,128)(2,1)S(1)}, bf16[512,1024]{1,0:T(8,128)(2,1)S(1)}, u32[]{:S(2)}, u32[]{:S(2)}) collective-permute-start(bf16[512,1024]{1,0:T(8,128)(2,1)S(1)} %collective-permute-done.21), channel_id=1, source_target_pairs={{0,8},{8,16},{16,24},{24,0},{1,9},{9,17},{17,25},{25,1},{2,10},{10... | collective-permute-start | bytes 3145736 | tf_op jit(solution)/shard_map/ppermute | solution.py:20
  154.6 3.3 broadcast_select_fusion.29
  159.4 17.6 %collective-permute-done.23 = bf16[512,1024]{1,0:T(8,128)(2,1)S(1)} collective-permute-done((bf16[512,1024]{1,0:T(8,128)(2,1)S(1)}, bf16[512,1024]{1,0:T(8,128)(2,1)S(1)}, u32[]{:S(2)}, u32[]{:S(2)}) %collective-permute-start.23) | collective-permute-done | bytes 1048608 | tf_op jit(solution)/shard_map/ppermute | solution.py:20
  179.7 6.7 %fusion.7 = f32[1792,1024]{0,1:T(8,128)} fusion(bf16[512,1024]{1,0:T(8,128)(2,1)S(1)} %get-tuple-element.29, bf16[512,1024]{1,0:T(8,128)(2,1)S(1)} %get-tuple-element.28, bf16[256,1792]{1,0:T(8,128)(2,1)S(1)} %get-tuple-element.19, bf16[256,1792]{1,0:T(8,128)(2,1)S(1)} %get-tuple-element.18, bf16[256,1792]{1,0:T(8,128)(2,1)S(1)} %get-tuple-element.17, ...), kind=kOutput, calls=%fused_computation.18 | convolution fusion | flops 3776970752 | bytes 13107200 | tf_op jit(solution)/shard_map/dot_general | solution.py:107
  186.4 14.6 %collective-permute-done.24 = bf16[512,1024]{1,0:T(8,128)(2,1)S(1)} collective-permute-done((bf16[512,1024]{1,0:T(8,128)(2,1)S(1)}, bf16[512,1024]{1,0:T(8,128)(2,1)S(1)}, u32[]{:S(2)}, u32[]{:S(2)}) %collective-permute-start.24) | collective-permute-done | bytes 1048608 | tf_op jit(solution)/shard_map/ppermute | solution.py:24
  202.4 13.7 %add_add_fusion = f32[1792,1024]{0,1:T(8,128)} fusion(f32[1792,1024]{0,1:T(8,128)} %fusion.7, f32[1792,1024]{0,1:T(8,128)} %fusion.1, f32[1792,1024]{0,1:T(8,128)} %fusion.3, bf16[512,1024]{1,0:T(8,128)(2,1)} %get-tuple-element.25, bf16[512,1024]{1,0:T(8,128)(2,1)} %get-tuple-element.24, bf16[256,1792]{1,0:T(8,128)(2,1)} %get-tuple-element.15, ...), kind=kOutput, calls=%fused_computation.5 | convolution fusion | flops 3782475776 | bytes 35127296 | tf_op jit(solution)/shard_map/dot_general | solution.py:107
  216.2 8.0 %multiply_reduce_fusion = (f32[1792]{0:T(1024)S(1)}, f32[1,1792,1024]{1,2,0:T(8,128)}, bf16[1792,1024]{0,1:T(8,128)(2,1)S(1)}) fusion(f32[1792,1024]{0,1:T(8,128)} %add_add_fusion, f32[1792]{0:T(1024)S(1)} %dynamic-slice_reduce_fusion, f32[1,1792,1024]{1,2,0:T(8,128)S(1)} %bitcast.20), kind=kLoop, calls=%fused_computation.4 | loop fusion | flops 29358336 | bytes 25704448 | tf_op jit(solution)/shard_map/reduce_sum | solution.py:113
  224.2 3.1 fusion.39
  227.7 5.1 %pad_maximum_fusion.1 = bf16[1024,1792]{1,0:T(8,128)(2,1)S(1)} fusion(bf16[256,1792]{1,0:T(8,128)(2,1)} %copy-done.14, bf16[256,1792]{1,0:T(8,128)(2,1)} %copy-done.13, bf16[256,1792]{1,0:T(8,128)(2,1)S(1)} %copy-done.12, bf16[256,1792]{1,0:T(8,128)(2,1)S(1)} %copy-done.10), kind=kLoop, calls=%fused_computation.10 | loop fusion | flops 14680064 | bytes 7340032 | tf_op jit(solution)/shard_map/concatenate | solution.py:43
  236.6 17.0 %collective-permute-done.15 = bf16[512,1024]{1,0:T(8,128)(2,1)} collective-permute-done((bf16[512,1024]{1,0:T(8,128)(2,1)}, bf16[512,1024]{1,0:T(8,128)(2,1)}, u32[]{:S(2)}, u32[]{:S(2)}) %collective-permute-start.15) | collective-permute-done | bytes 1048608 | tf_op jit(solution)/shard_map/ppermute | solution.py:24
  253.6 3.3 %add_convert_fusion.3 = bf16[512,1024]{1,0:T(8,128)(2,1)S(1)} fusion(bf16[512,1024]{1,0:T(8,128)(2,1)} %collective-permute-done.15, bf16[1792,1024]{0,1:T(8,128)(2,1)S(1)} %copy-done.16, bf16[1024,1792]{1,0:T(8,128)(2,1)S(1)} %copy-done.3, s32[]{:T(128)S(6)} %select_n.214), kind=kOutput, calls=%fused_computation.28 | convolution fusion | flops 1880621056 | bytes 7602180 | tf_op jit(solution)/shard_map/dot_general | solution.py:82
  259.9 3.1 fusion.33
  263.6 12.4 %collective-permute-done.10 = bf16[512,1024]{1,0:T(8,128)(2,1)S(1)} collective-permute-done((bf16[512,1024]{1,0:T(8,128)(2,1)S(1)}, bf16[512,1024]{1,0:T(8,128)(2,1)S(1)}, u32[]{:S(2)}, u32[]{:S(2)}) %collective-permute-start.10) | collective-permute-done | bytes 1048608 | tf_op jit(solution)/shard_map/ppermute | solution.py:24
  275.9 3.7 %collective-permute-done.16 = bf16[512,1024]{1,0:T(8,128)(2,1)S(1)} collective-permute-done((bf16[512,1024]{1,0:T(8,128)(2,1)S(1)}, bf16[512,1024]{1,0:T(8,128)(2,1)S(1)}, u32[]{:S(2)}, u32[]{:S(2)}) %collective-permute-start.16) | collective-permute-done | bytes 1048608 | tf_op jit(solution)/shard_map/ppermute | solution.py:20
  279.7 3.1 add_convert_fusion.2
  282.8 5.9 %fusion.30 = bf16[512,1024]{1,0:T(8,128)(2,1)} fusion(bf16[1792,1024]{0,1:T(8,128)(2,1)} %copy-done.15, bf16[1024,7168]{1,0:T(8,128)(2,1)} %param.5, s32[]{:T(128)S(6)} %select_n.219, s32[]{:T(128)S(6)} %select_n.217), kind=kOutput, calls=%fused_computation.45 | convolution fusion | flops 1879572480 | bytes 6553608 | tf_op jit(solution)/shard_map/dot_general | solution.py:80
  289.2 9.2 %collective-permute-done.5 = bf16[512,1024]{1,0:T(8,128)(2,1)S(1)} collective-permute-done((bf16[512,1024]{1,0:T(8,128)(2,1)}, bf16[512,1024]{1,0:T(8,128)(2,1)S(1)}, u32[]{:S(2)}, u32[]{:S(2)}) %collective-permute-start.5) | collective-permute-done | bytes 1048608 | tf_op jit(solution)/shard_map/ppermute | solution.py:24
  298.4 5.7 %collective-permute-done.17 = bf16[512,1024]{1,0:T(8,128)(2,1)S(1)} collective-permute-done((bf16[512,1024]{1,0:T(8,128)(2,1)}, bf16[512,1024]{1,0:T(8,128)(2,1)S(1)}, u32[]{:S(2)}, u32[]{:S(2)}) %collective-permute-start.17) | collective-permute-done | bytes 1048608 | tf_op jit(solution)/shard_map/ppermute | solution.py:20
  304.2 3.1 add_convert_fusion.1
  307.3 8.4 %copy.8 = f32[1,1792,1024]{2,1,0:T(8,128)} copy(f32[1,1792,1024]{1,2,0:T(8,128)} %get-tuple-element.7) | data formatting | bytes 14680064
  315.7 6.7 %psum.7 = f32[1,1792]{1,0:T(1,128)} all-reduce(f32[1,1792]{1,0:T(1,128)S(1)} %broadcast_in_dim.19), channel_id=1, replica_groups=mesh['dp'=4,'row'=2,'col'=4] {'col'}, use_global_device_ids=true, to_apply=%region_1.2 | all-reduce | flops 1792 | bytes 14336 | tf_op jit(solution)/shard_map/psum | solution.py:113
  322.4 4.9 %fusion.28 = f32[512,1024]{1,0:T(8,128)S(1)} fusion(bf16[1792,1024]{0,1:T(8,128)(2,1)} %copy-done.15, bf16[1024,7168]{1,0:T(8,128)(2,1)} %param.5, s32[]{:T(128)S(6)} %select_n.215, s32[]{:T(128)S(6)} %select_n.217), kind=kOutput, calls=%fused_computation.43 | convolution fusion | flops 1879048192 | bytes 7602184 | tf_op jit(solution)/shard_map/dot_general | solution.py:82
  (90 shorter events, 39.0 us)
Async XLA Ops:
  3.3 29.3 %collective-permute-start.19 = (bf16[512,1024]{1,0:T(8,128)(2,1)}, bf16[512,1024]{1,0:T(8,128)(2,1)S(1)}, u32[]{:S(2)}, u32[]{:S(2)}) collective-permute-start(bf16[512,1024]{1,0:T(8,128)(2,1)} %constant_dynamic-slice_fusion), channel_id=1, source_target_pairs={{0,8},{8,16},{16,24},{24,0},{1,9},{9,17},{17,25},{25,1},{2,10},{10... | collective-permute-start | bytes 3145736 | tf_op jit(solution)/shard_map/ppermute | solution.py:20
  11.0 41.4 %collective-permute-start.11 = (bf16[256,1792]{1,0:T(8,128)(2,1)S(1)}, bf16[256,1792]{1,0:T(8,128)(2,1)}, u32[]{:S(2)}, u32[]{:S(2)}) collective-permute-start(bf16[256,1792]{1,0:T(8,128)(2,1)S(1)} %get-tuple-element.10), channel_id=1, source_target_pairs={{0,8},{8,16},{16,24},{24,0},{1,9},{9,17},{17,25},{25,1},{2,10},{10... | collective-permute-start | bytes 2752520 | tf_op jit(solution)/shard_map/ppermute | solution.py:20
  32.6 79.4 %collective-permute-start.20 = (bf16[512,1024]{1,0:T(8,128)(2,1)S(1)}, bf16[512,1024]{1,0:T(8,128)(2,1)}, u32[]{:S(2)}, u32[]{:S(2)}) collective-permute-start(bf16[512,1024]{1,0:T(8,128)(2,1)S(1)} %collective-permute-done.19), channel_id=1, source_target_pairs={{0,4},{4,0},{1,5},{5,1},{2,6},{6,2},{3,7},{7,3},{8,12},{12,8},{9,1... | collective-permute-start | bytes 3145736 | tf_op jit(solution)/shard_map/ppermute | solution.py:24
  34.3 36.9 %collective-permute-start.1 = (bf16[256,1792]{1,0:T(8,128)(2,1)}, bf16[256,1792]{1,0:T(8,128)(2,1)}, u32[]{:S(2)}, u32[]{:S(2)}) collective-permute-start(bf16[256,1792]{1,0:T(8,128)(2,1)} %get-tuple-element.8), channel_id=1, source_target_pairs={{0,24},{8,0},{16,8},{24,16},{1,25},{9,1},{17,9},{25,17},{2,26},{10... | collective-permute-start | bytes 2752520 | tf_op jit(solution)/shard_map/ppermute | solution.py:20
  36.1 74.4 %collective-permute-start.6 = (bf16[256,1792]{1,0:T(8,128)(2,1)}, bf16[256,1792]{1,0:T(8,128)(2,1)}, u32[]{:S(2)}, u32[]{:S(2)}) collective-permute-start(bf16[256,1792]{1,0:T(8,128)(2,1)} %get-tuple-element.9), channel_id=1, source_target_pairs={{0,16},{8,24},{16,0},{24,8},{1,17},{9,25},{17,1},{25,9},{2,18},{10... | collective-permute-start | bytes 2752520 | tf_op jit(solution)/shard_map/ppermute | solution.py:20
  52.4 59.6 %collective-permute-start.12 = (bf16[256,1792]{1,0:T(8,128)(2,1)}, bf16[256,1792]{1,0:T(8,128)(2,1)}, u32[]{:S(2)}, u32[]{:S(2)}) collective-permute-start(bf16[256,1792]{1,0:T(8,128)(2,1)} %collective-permute-done.11), channel_id=1, source_target_pairs={{0,2},{1,3},{2,0},{3,1},{4,6},{5,7},{6,4},{7,5},{8,10},{9,11},{10,... | collective-permute-start | bytes 2752520 | tf_op jit(solution)/shard_map/ppermute | solution.py:24
  63.3 58.9 %collective-permute-start.14 = (bf16[256,1792]{1,0:T(8,128)(2,1)}, bf16[256,1792]{1,0:T(8,128)(2,1)S(1)}, u32[]{:S(2)}, u32[]{:S(2)}) collective-permute-start(bf16[256,1792]{1,0:T(8,128)(2,1)} %collective-permute-done.11), channel_id=1, source_target_pairs={{0,1},{1,0},{2,3},{3,2},{4,5},{5,4},{6,7},{7,6},{8,9},{9,8},{10,11... | collective-permute-start | bytes 2752520 | tf_op jit(solution)/shard_map/ppermute | solution.py:24
  71.2 50.4 %collective-permute-start.2 = (bf16[256,1792]{1,0:T(8,128)(2,1)}, bf16[256,1792]{1,0:T(8,128)(2,1)S(1)}, u32[]{:S(2)}, u32[]{:S(2)}) collective-permute-start(bf16[256,1792]{1,0:T(8,128)(2,1)} %collective-permute-done.1), channel_id=1, source_target_pairs={{0,2},{1,3},{2,0},{3,1},{4,6},{5,7},{6,4},{7,5},{8,10},{9,11},{10,... | collective-permute-start | bytes 2752520 | tf_op jit(solution)/shard_map/ppermute | solution.py:24
  110.5 22.4 %collective-permute-start.7 = (bf16[256,1792]{1,0:T(8,128)(2,1)}, bf16[256,1792]{1,0:T(8,128)(2,1)S(1)}, u32[]{:S(2)}, u32[]{:S(2)}) collective-permute-start(bf16[256,1792]{1,0:T(8,128)(2,1)} %collective-permute-done.6), channel_id=1, source_target_pairs={{0,2},{1,3},{2,0},{3,1},{4,6},{5,7},{6,4},{7,5},{8,10},{9,11},{10,... | collective-permute-start | bytes 2752520 | tf_op jit(solution)/shard_map/ppermute | solution.py:24
  112.0 26.6 %collective-permute-start.21 = (bf16[512,1024]{1,0:T(8,128)(2,1)S(1)}, bf16[512,1024]{1,0:T(8,128)(2,1)S(1)}, u32[]{:S(2)}, u32[]{:S(2)}) collective-permute-start(bf16[512,1024]{1,0:T(8,128)(2,1)S(1)} %collective-permute-done.19), channel_id=1, source_target_pairs={{0,8},{8,16},{16,24},{24,0},{1,9},{9,17},{17,25},{25,1},{2,10},{10... | collective-permute-start | bytes 3145736 | tf_op jit(solution)/shard_map/ppermute | solution.py:20
  112.0 26.6 %collective-permute-start.13 = (bf16[256,1792]{1,0:T(8,128)(2,1)}, bf16[256,1792]{1,0:T(8,128)(2,1)S(1)}, u32[]{:S(2)}, u32[]{:S(2)}) collective-permute-start(bf16[256,1792]{1,0:T(8,128)(2,1)} %collective-permute-done.12), channel_id=1, source_target_pairs={{0,1},{1,0},{2,3},{3,2},{4,5},{5,4},{6,7},{7,6},{8,9},{9,8},{10,11... | collective-permute-start | bytes 2752520 | tf_op jit(solution)/shard_map/ppermute | solution.py:24
  121.6 27.0 %collective-permute-start.4 = (bf16[256,1792]{1,0:T(8,128)(2,1)}, bf16[256,1792]{1,0:T(8,128)(2,1)S(1)}, u32[]{:S(2)}, u32[]{:S(2)}) collective-permute-start(bf16[256,1792]{1,0:T(8,128)(2,1)} %collective-permute-done.1), channel_id=1, source_target_pairs={{0,1},{1,0},{2,3},{3,2},{4,5},{5,4},{6,7},{7,6},{8,9},{9,8},{10,11... | collective-permute-start | bytes 2752520 | tf_op jit(solution)/shard_map/ppermute | solution.py:24
  122.2 35.7 %collective-permute-start.9 = (bf16[256,1792]{1,0:T(8,128)(2,1)}, bf16[256,1792]{1,0:T(8,128)(2,1)S(1)}, u32[]{:S(2)}, u32[]{:S(2)}) collective-permute-start(bf16[256,1792]{1,0:T(8,128)(2,1)} %collective-permute-done.6), channel_id=1, source_target_pairs={{0,1},{1,0},{2,3},{3,2},{4,5},{5,4},{6,7},{7,6},{8,9},{9,8},{10,11... | collective-permute-start | bytes 2752520 | tf_op jit(solution)/shard_map/ppermute | solution.py:24
  132.9 21.7 %collective-permute-start.3 = (bf16[256,1792]{1,0:T(8,128)(2,1)S(1)}, bf16[256,1792]{1,0:T(8,128)(2,1)S(1)}, u32[]{:S(2)}, u32[]{:S(2)}) collective-permute-start(bf16[256,1792]{1,0:T(8,128)(2,1)S(1)} %collective-permute-done.2), channel_id=1, source_target_pairs={{0,1},{1,0},{2,3},{3,2},{4,5},{5,4},{6,7},{7,6},{8,9},{9,8},{10,11... | collective-permute-start | bytes 2752520 | tf_op jit(solution)/shard_map/ppermute | solution.py:24
  138.5 19.4 %collective-permute-start.8 = (bf16[256,1792]{1,0:T(8,128)(2,1)S(1)}, bf16[256,1792]{1,0:T(8,128)(2,1)S(1)}, u32[]{:S(2)}, u32[]{:S(2)}) collective-permute-start(bf16[256,1792]{1,0:T(8,128)(2,1)S(1)} %collective-permute-done.7), channel_id=1, source_target_pairs={{0,1},{1,0},{2,3},{3,2},{4,5},{5,4},{6,7},{7,6},{8,9},{9,8},{10,11... | collective-permute-start | bytes 2752520 | tf_op jit(solution)/shard_map/ppermute | solution.py:24
  138.5 41.0 %collective-permute-start.22 = (bf16[512,1024]{1,0:T(8,128)(2,1)S(1)}, bf16[512,1024]{1,0:T(8,128)(2,1)S(1)}, u32[]{:S(2)}, u32[]{:S(2)}) collective-permute-start(bf16[512,1024]{1,0:T(8,128)(2,1)S(1)} %collective-permute-done.21), channel_id=1, source_target_pairs={{0,4},{4,0},{1,5},{5,1},{2,6},{6,2},{3,7},{7,3},{8,12},{12,8},{9,1... | collective-permute-start | bytes 3145736 | tf_op jit(solution)/shard_map/ppermute | solution.py:24
  148.6 28.3 %collective-permute-start.23 = (bf16[512,1024]{1,0:T(8,128)(2,1)S(1)}, bf16[512,1024]{1,0:T(8,128)(2,1)S(1)}, u32[]{:S(2)}, u32[]{:S(2)}) collective-permute-start(bf16[512,1024]{1,0:T(8,128)(2,1)S(1)} %collective-permute-done.21), channel_id=1, source_target_pairs={{0,8},{8,16},{16,24},{24,0},{1,9},{9,17},{17,25},{25,1},{2,10},{10... | collective-permute-start | bytes 3145736 | tf_op jit(solution)/shard_map/ppermute | solution.py:20
  159.4 20.3 %copy-start.9 = (bf16[256,1792]{1,0:T(8,128)(2,1)}, bf16[256,1792]{1,0:T(8,128)(2,1)S(1)}, u32[]{:S(2)}) copy-start(bf16[256,1792]{1,0:T(8,128)(2,1)S(1)} %get-tuple-element.16) | copy-start | bytes 2752516
  177.0 24.0 %collective-permute-start.24 = (bf16[512,1024]{1,0:T(8,128)(2,1)S(1)}, bf16[512,1024]{1,0:T(8,128)(2,1)S(1)}, u32[]{:S(2)}, u32[]{:S(2)}) collective-permute-start(bf16[512,1024]{1,0:T(8,128)(2,1)S(1)} %collective-permute-done.23), channel_id=1, source_target_pairs={{0,4},{4,0},{1,5},{5,1},{2,6},{6,2},{3,7},{7,3},{8,12},{12,8},{9,1... | collective-permute-start | bytes 3145736 | tf_op jit(solution)/shard_map/ppermute | solution.py:24
  227.2 26.4 %collective-permute-start.15 = (bf16[512,1024]{1,0:T(8,128)(2,1)}, bf16[512,1024]{1,0:T(8,128)(2,1)}, u32[]{:S(2)}, u32[]{:S(2)}) collective-permute-start(bf16[512,1024]{1,0:T(8,128)(2,1)} %fusion.39), channel_id=1, source_target_pairs={{0,4},{4,0},{1,5},{5,1},{2,6},{6,2},{3,7},{7,3},{8,12},{12,8},{9,1... | collective-permute-start | bytes 3145736 | tf_op jit(solution)/shard_map/ppermute | solution.py:24
  232.9 20.7 %copy-start.3 = (bf16[1024,1792]{1,0:T(8,128)(2,1)S(1)}, bf16[1024,1792]{1,0:T(8,128)(2,1)}, u32[]{:S(2)}) copy-start(bf16[1024,1792]{1,0:T(8,128)(2,1)} %pad_maximum_fusion.2) | copy-start | bytes 11010052
  235.0 24.6 %copy-start.6 = (bf16[256,1792]{1,0:T(8,128)(2,1)S(1)}, bf16[256,1792]{1,0:T(8,128)(2,1)}, u32[]{:S(2)}) copy-start(bf16[256,1792]{1,0:T(8,128)(2,1)} %get-tuple-element.13) | copy-start | bytes 2752516
  235.0 24.5 %copy-start.7 = (bf16[256,1792]{1,0:T(8,128)(2,1)S(1)}, bf16[256,1792]{1,0:T(8,128)(2,1)}, u32[]{:S(2)}) copy-start(bf16[256,1792]{1,0:T(8,128)(2,1)} %get-tuple-element.14) | copy-start | bytes 2752516
  235.0 24.5 %copy-start.8 = (bf16[256,1792]{1,0:T(8,128)(2,1)S(1)}, bf16[256,1792]{1,0:T(8,128)(2,1)}, u32[]{:S(2)}) copy-start(bf16[256,1792]{1,0:T(8,128)(2,1)} %get-tuple-element.15) | copy-start | bytes 2752516
  235.0 40.9 %collective-permute-start.10 = (bf16[512,1024]{1,0:T(8,128)(2,1)S(1)}, bf16[512,1024]{1,0:T(8,128)(2,1)S(1)}, u32[]{:S(2)}, u32[]{:S(2)}) collective-permute-start(bf16[512,1024]{1,0:T(8,128)(2,1)S(1)} %fusion.36), channel_id=1, source_target_pairs={{0,4},{4,0},{1,5},{5,1},{2,6},{6,2},{3,7},{7,3},{8,12},{12,8},{9,1... | collective-permute-start | bytes 3145736 | tf_op jit(solution)/shard_map/ppermute | solution.py:24
  256.9 22.8 %collective-permute-start.16 = (bf16[512,1024]{1,0:T(8,128)(2,1)S(1)}, bf16[512,1024]{1,0:T(8,128)(2,1)S(1)}, u32[]{:S(2)}, u32[]{:S(2)}) collective-permute-start(bf16[512,1024]{1,0:T(8,128)(2,1)S(1)} %add_convert_fusion.3), channel_id=1, source_target_pairs={{0,8},{8,16},{16,24},{24,0},{1,9},{9,17},{17,25},{25,1},{2,10},{10... | collective-permute-start | bytes 3145736 | tf_op jit(solution)/shard_map/ppermute | solution.py:20
  263.1 35.4 %collective-permute-start.5 = (bf16[512,1024]{1,0:T(8,128)(2,1)}, bf16[512,1024]{1,0:T(8,128)(2,1)S(1)}, u32[]{:S(2)}, u32[]{:S(2)}) collective-permute-start(bf16[512,1024]{1,0:T(8,128)(2,1)} %fusion.33), channel_id=1, source_target_pairs={{0,4},{4,0},{1,5},{5,1},{2,6},{6,2},{3,7},{7,3},{8,12},{12,8},{9,1... | collective-permute-start | bytes 3145736 | tf_op jit(solution)/shard_map/ppermute | solution.py:24
  282.8 21.4 %collective-permute-start.17 = (bf16[512,1024]{1,0:T(8,128)(2,1)}, bf16[512,1024]{1,0:T(8,128)(2,1)S(1)}, u32[]{:S(2)}, u32[]{:S(2)}) collective-permute-start(bf16[512,1024]{1,0:T(8,128)(2,1)} %add_convert_fusion.2), channel_id=1, source_target_pairs={{0,8},{8,16},{16,24},{24,0},{1,9},{9,17},{17,25},{25,1},{2,10},{10... | collective-permute-start | bytes 3145736 | tf_op jit(solution)/shard_map/ppermute | solution.py:20
  282.8 21.4 %copy-start.5 = (bf16[1024,1792]{1,0:T(8,128)(2,1)S(1)}, bf16[1024,1792]{1,0:T(8,128)(2,1)}, u32[]{:S(2)}) copy-start(bf16[1024,1792]{1,0:T(8,128)(2,1)} %copy-done.4) | copy-start | bytes 11010052
  282.8 21.4 %copy-start.17 = (bf16[1792,1024]{0,1:T(8,128)(2,1)S(1)}, bf16[1792,1024]{0,1:T(8,128)(2,1)}, u32[]{:S(2)}) copy-start(bf16[1792,1024]{0,1:T(8,128)(2,1)} %copy-done.15) | copy-start | bytes 11010052
  288.7 38.6 %collective-permute-start = (bf16[512,1024]{1,0:T(8,128)(2,1)}, bf16[512,1024]{1,0:T(8,128)(2,1)S(1)}, u32[]{:S(2)}, u32[]{:S(2)}) collective-permute-start(bf16[512,1024]{1,0:T(8,128)(2,1)} %fusion.30), channel_id=1, source_target_pairs={{0,4},{4,0},{1,5},{5,1},{2,6},{6,2},{3,7},{7,3},{8,12},{12,8},{9,1... | collective-permute-start | bytes 3145736 | tf_op jit(solution)/shard_map/ppermute | solution.py:24
  307.3 20.6 %collective-permute-start.18 = (bf16[512,1024]{1,0:T(8,128)(2,1)}, bf16[512,1024]{1,0:T(8,128)(2,1)}, u32[]{:S(2)}, u32[]{:S(2)}) collective-permute-start(bf16[512,1024]{1,0:T(8,128)(2,1)} %add_convert_fusion.1), channel_id=1, source_target_pairs={{0,8},{8,16},{16,24},{24,0},{1,9},{9,17},{17,25},{25,1},{2,10},{10... | collective-permute-start | bytes 3145736 | tf_op jit(solution)/shard_map/ppermute | solution.py:20
  (13 other events, 126.2 us)
where the time goes:
time: 331 us
  waiting for transfers between devices  179 us (54%)
  matrix products  64 us (19%)
  other arithmetic  27.8 us (8%)
  starting transfers between devices  27.4 us (8%)
  local copies, waits for them, and re-layouts  24.9 us (8%)
  blocking collectives  6.73 us (2%)
    ppermute x9, waiting for transfers between devices, shift(): lax.ppermute(block, axis, [(i, (i + by) % count) for i in range(count)])  115 us
    ppermute x16, waiting for transfers between devices, swap(): return lax.ppermute(block, axis, [(i, i ^ bit) for i in range(count)])  63.8 us
    dot_general x3, matrix products, shards(): lax.dot_general(grad, act, (((0,), (0,)), ((), ())), preferred_element_ty...  27.1 us
    unnamed x42, local copies, waits for them, and re-layouts  18.4 us
    ppermute x9, starting transfers between devices, shift(): lax.ppermute(block, axis, [(i, (i + by) % count) for i in range(count)])  15 us
    dot_general x4, matrix products, reduced(): jnp.dot(kept, quantized, preferred_element_type=jnp.float32)  14.5 us
    dot_general x4, matrix products, reduced(): jnp.dot(sent, quantized, preferred_element_type=jnp.float32)  14.2 us
    ppermute x16, starting transfers between devices, swap(): return lax.ppermute(block, axis, [(i, i ^ bit) for i in range(count)])  12.3 us
  transfers between devices with their start and end apart: 25, of which 14 were waited for; matrix products, arithmetic and copies ran while one was open for 26% of the time, Pallas kernels for 0%

commit v1 on v0

--- a/solution.py
+++ b/solution.py
@@ -110,7 +110,9 @@
         if running is not None:
             own_total = own_total + running.astype(jnp.float32)
         input_grad = own_total.astype(jnp.bfloat16)
-        step_rows = lax.psum(jnp.sum(products * factor, axis=1) * grad_factor, "col")
+        x = jnp.sum(products * factor, axis=1) * grad_factor
+        blocks = lax.all_gather(x, "col", axis=0, tiled=False)
+        step_rows = blocks.sum(axis=0)
         weight_grad = (products * inside)[None]
         return (input_grad, weight_grad, step_rows[None])
 

time: 331 us -> 331 us (level)
    psum x1 -> x0, blocking collectives: 6.73 us -> none  [shards(): lax.psum(jnp.sum(products * factor, axis=1) * grad_factor, 'col')]
    all_gather x0 -> x1, blocking collectives: none -> 5.22 us  [shards(): blocks = lax.all_gather(x, 'col', axis=0, tiled=False)]
    reduce_sum x1 -> x2, other arithmetic: 7.96 us -> 8 us  [the longest x1 7.96 us: shards(): x = jnp.sum(products * factor, axis=1) * grad_factor]
    unnamed x42 -> x43, local copies, waits for them, and re-layouts: 18.4 us -> 18.5 us
where the time goes in v1:
time: 331 us
  waiting for transfers between devices  180 us (54%)
  matrix products  64 us (19%)
  other arithmetic  27.8 us (8%)
  starting transfers between devices  27.4 us (8%)
  local copies, waits for them, and re-layouts  25.5 us (8%)
  blocking collectives  5.22 us (2%)
    ppermute x9, waiting for transfers between devices, shift(): lax.ppermute(block, axis, [(i, (i + by) % count) for i in range(count)])  116 us
    ppermute x16, waiting for transfers between devices, swap(): return lax.ppermute(block, axis, [(i, i ^ bit) for i in range(count)])  63.8 us
    dot_general x3, matrix products, shards(): lax.dot_general(grad, act, (((0,), (0,)), ((), ())), preferred_element_ty...  27.1 us
    unnamed x43, local copies, waits for them, and re-layouts  18.5 us
    ppermute x9, starting transfers between devices, shift(): lax.ppermute(block, axis, [(i, (i + by) % count) for i in range(count)])  15 us
    dot_general x4, matrix products, reduced(): jnp.dot(kept, quantized, preferred_element_type=jnp.float32)  14.5 us
    dot_general x4, matrix products, reduced(): jnp.dot(sent, quantized, preferred_element_type=jnp.float32)  14.2 us
    ppermute x16, starting transfers between devices, swap(): return lax.ppermute(block, axis, [(i, i ^ bit) for i in range(count)])  12.3 us
  transfers between devices with their start and end apart: 25, of which 14 were waited for; matrix products, arithmetic and copies ran while one was open for 26% of the time, Pallas kernels for 0%

profile of v1, /device:TPU:0, one launch (start us, length us, event | category | flops | bytes accessed | tf_op | source)
XLA Modules:
  0.0 330.7 jit_solution(12303775881280463528)
XLA Ops:
  6.3 4.7 %fusion.58 = (bf16[256,1792]{1,0:T(8,128)(2,1)}, bf16[256,1792]{1,0:T(8,128)(2,1)}, bf16[256,1792]{1,0:T(8,128)(2,1)S(1)}) fusion(bf16[1024,7168]{1,0:T(8,128)(2,1)} %param.5, s32[]{:T(128)S(6)} %select_n.223, s32[]{:T(128)S(6)} %select_n.226, s32[]{:T(128)S(6)} %select_n.237, s32[]{:T(128)S(6)} %select_n.248), kind=kLoop, calls=%fused_computation.92 | loop fusion | bytes 5505040 | tf_op jit(solution)/shard_map/dynamic_slice | solution.py:64
  12.6 20.0 %collective-permute-done.19 = bf16[512,1024]{1,0:T(8,128)(2,1)S(1)} collective-permute-done((bf16[512,1024]{1,0:T(8,128)(2,1)}, bf16[512,1024]{1,0:T(8,128)(2,1)S(1)}, u32[]{:S(2)}, u32[]{:S(2)}) %collective-permute-start.19) | collective-permute-done | bytes 1048608 | tf_op jit(solution)/shard_map/ppermute | solution.py:20
  36.1 16.3 %collective-permute-done.11 = bf16[256,1792]{1,0:T(8,128)(2,1)} collective-permute-done((bf16[256,1792]{1,0:T(8,128)(2,1)S(1)}, bf16[256,1792]{1,0:T(8,128)(2,1)}, u32[]{:S(2)}, u32[]{:S(2)}) %collective-permute-start.11) | collective-permute-done | bytes 917536 | tf_op jit(solution)/shard_map/ppermute | solution.py:20
  54.1 8.4 %copy.9 = f32[1,1792,1024]{1,2,0:T(8,128)} copy(f32[1,1792,1024]{2,1,0:T(8,128)} %param.6) | data formatting | bytes 14680064 | tf_op args[2]
  63.3 7.9 %collective-permute-done.1 = bf16[256,1792]{1,0:T(8,128)(2,1)} collective-permute-done((bf16[256,1792]{1,0:T(8,128)(2,1)}, bf16[256,1792]{1,0:T(8,128)(2,1)}, u32[]{:S(2)}, u32[]{:S(2)}) %collective-permute-start.1) | collective-permute-done | bytes 917536 | tf_op jit(solution)/shard_map/ppermute | solution.py:20
  72.7 37.7 %collective-permute-done.6 = bf16[256,1792]{1,0:T(8,128)(2,1)} collective-permute-done((bf16[256,1792]{1,0:T(8,128)(2,1)}, bf16[256,1792]{1,0:T(8,128)(2,1)}, u32[]{:S(2)}, u32[]{:S(2)}) %collective-permute-start.6) | collective-permute-done | bytes 917536 | tf_op jit(solution)/shard_map/ppermute | solution.py:20
  112.0 8.2 %fusion.1 = f32[1792,1024]{0,1:T(8,128)} fusion(bf16[1024,1024]{1,0:T(8,128)(2,1)S(1)} %copy-done, bf16[1024,7168]{1,0:T(8,128)(2,1)} %param.5, s32[]{:T(128)S(6)} %select_n.216), kind=kOutput, calls=%fused_computation.12 | convolution fusion | flops 3758096384 | bytes 13107204 | tf_op jit(solution)/shard_map/dot_general | solution.py:95
  122.3 10.7 %collective-permute-done.7 = bf16[256,1792]{1,0:T(8,128)(2,1)S(1)} collective-permute-done((bf16[256,1792]{1,0:T(8,128)(2,1)}, bf16[256,1792]{1,0:T(8,128)(2,1)S(1)}, u32[]{:S(2)}, u32[]{:S(2)}) %collective-permute-start.7) | collective-permute-done | bytes 917536 | tf_op jit(solution)/shard_map/ppermute | solution.py:24
  132.9 5.6 %collective-permute-done.21 = bf16[512,1024]{1,0:T(8,128)(2,1)S(1)} collective-permute-done((bf16[512,1024]{1,0:T(8,128)(2,1)S(1)}, bf16[512,1024]{1,0:T(8,128)(2,1)S(1)}, u32[]{:S(2)}, u32[]{:S(2)}) %collective-permute-start.21) | collective-permute-done | bytes 1048608 | tf_op jit(solution)/shard_map/ppermute | solution.py:20
  141.9 6.7 %fusion.3 = f32[1792,1024]{0,1:T(8,128)} fusion(bf16[512,1024]{1,0:T(8,128)(2,1)S(1)} %get-tuple-element.30, bf16[512,1024]{1,0:T(8,128)(2,1)S(1)} %get-tuple-element.29, bf16[256,1792]{1,0:T(8,128)(2,1)S(1)} %get-tuple-element.26, bf16[256,1792]{1,0:T(8,128)(2,1)S(1)} %get-tuple-element.25, bf16[256,1792]{1,0:T(8,128)(2,1)S(1)} %get-tuple-element.24, ...), kind=kOutput, calls=%fused_computation.14 | convolution fusion | flops 3776970752 | bytes 13107200 | tf_op jit(solution)/shard_map/dot_general | solution.py:107
  148.6 6.0 %collective-permute-start.23 = (bf16[512,1024]{1,0:T(8,128)(2,1)S(1)}, bf16[512,1024]{1,0:T(8,128)(2,1)S(1)}, u32[]{:S(2)}, u32[]{:S(2)}) collective-permute-start(bf16[512,1024]{1,0:T(8,128)(2,1)S(1)} %collective-permute-done.21), channel_id=1, source_target_pairs={{0,8},{8,16},{16,24},{24,0},{1,9},{9,17},{17,25},{25,1},{2,10},{10... | collective-permute-start | bytes 3145736 | tf_op jit(solution)/shard_map/ppermute | solution.py:20
  154.6 3.3 broadcast_select_fusion.29
  159.4 17.6 %collective-permute-done.23 = bf16[512,1024]{1,0:T(8,128)(2,1)S(1)} collective-permute-done((bf16[512,1024]{1,0:T(8,128)(2,1)S(1)}, bf16[512,1024]{1,0:T(8,128)(2,1)S(1)}, u32[]{:S(2)}, u32[]{:S(2)}) %collective-permute-start.23) | collective-permute-done | bytes 1048608 | tf_op jit(solution)/shard_map/ppermute | solution.py:20
  179.7 6.7 %fusion.7 = f32[1792,1024]{0,1:T(8,128)} fusion(bf16[512,1024]{1,0:T(8,128)(2,1)S(1)} %get-tuple-element.32, bf16[512,1024]{1,0:T(8,128)(2,1)S(1)} %get-tuple-element.31, bf16[256,1792]{1,0:T(8,128)(2,1)S(1)} %get-tuple-element.22, bf16[256,1792]{1,0:T(8,128)(2,1)S(1)} %get-tuple-element.21, bf16[256,1792]{1,0:T(8,128)(2,1)S(1)} %get-tuple-element.20, ...), kind=kOutput, calls=%fused_computation.18 | convolution fusion | flops 3776970752 | bytes 13107200 | tf_op jit(solution)/shard_map/dot_general | solution.py:107
  186.4 14.6 %collective-permute-done.24 = bf16[512,1024]{1,0:T(8,128)(2,1)S(1)} collective-permute-done((bf16[512,1024]{1,0:T(8,128)(2,1)S(1)}, bf16[512,1024]{1,0:T(8,128)(2,1)S(1)}, u32[]{:S(2)}, u32[]{:S(2)}) %collective-permute-start.24) | collective-permute-done | bytes 1048608 | tf_op jit(solution)/shard_map/ppermute | solution.py:24
  202.4 13.7 %add_add_fusion = f32[1792,1024]{0,1:T(8,128)} fusion(f32[1792,1024]{0,1:T(8,128)} %fusion.7, f32[1792,1024]{0,1:T(8,128)} %fusion.1, f32[1792,1024]{0,1:T(8,128)} %fusion.3, bf16[512,1024]{1,0:T(8,128)(2,1)} %get-tuple-element.28, bf16[512,1024]{1,0:T(8,128)(2,1)} %get-tuple-element.27, bf16[256,1792]{1,0:T(8,128)(2,1)} %get-tuple-element.18, ...), kind=kOutput, calls=%fused_computation.5 | convolution fusion | flops 3782475776 | bytes 35127296 | tf_op jit(solution)/shard_map/dot_general | solution.py:107
  216.2 8.0 %multiply_reduce_fusion = (f32[1792]{0:T(1024)S(1)}, f32[1,1792,1024]{1,2,0:T(8,128)}, bf16[1792,1024]{0,1:T(8,128)(2,1)S(1)}) fusion(f32[1792,1024]{0,1:T(8,128)} %add_add_fusion, f32[1792]{0:T(1024)S(1)} %dynamic-slice_reduce_fusion, f32[1,1792,1024]{1,2,0:T(8,128)S(1)} %bitcast.20), kind=kLoop, calls=%fused_computation.4 | loop fusion | flops 29358336 | bytes 25704448 | tf_op jit(solution)/shard_map/reduce_sum | solution.py:113
  224.2 3.1 fusion.39
  227.7 5.1 %pad_maximum_fusion.1 = bf16[1024,1792]{1,0:T(8,128)(2,1)S(1)} fusion(bf16[256,1792]{1,0:T(8,128)(2,1)} %copy-done.14, bf16[256,1792]{1,0:T(8,128)(2,1)} %copy-done.13, bf16[256,1792]{1,0:T(8,128)(2,1)S(1)} %copy-done.12, bf16[256,1792]{1,0:T(8,128)(2,1)S(1)} %copy-done.10), kind=kLoop, calls=%fused_computation.10 | loop fusion | flops 14680064 | bytes 7340032 | tf_op jit(solution)/shard_map/concatenate | solution.py:43
  236.6 17.0 %collective-permute-done.15 = bf16[512,1024]{1,0:T(8,128)(2,1)} collective-permute-done((bf16[512,1024]{1,0:T(8,128)(2,1)}, bf16[512,1024]{1,0:T(8,128)(2,1)}, u32[]{:S(2)}, u32[]{:S(2)}) %collective-permute-start.15) | collective-permute-done | bytes 1048608 | tf_op jit(solution)/shard_map/ppermute | solution.py:24
  253.6 3.3 %add_convert_fusion.3 = bf16[512,1024]{1,0:T(8,128)(2,1)S(1)} fusion(bf16[512,1024]{1,0:T(8,128)(2,1)} %collective-permute-done.15, bf16[1792,1024]{0,1:T(8,128)(2,1)S(1)} %copy-done.16, bf16[1024,1792]{1,0:T(8,128)(2,1)S(1)} %copy-done.3, s32[]{:T(128)S(6)} %select_n.214), kind=kOutput, calls=%fused_computation.28 | convolution fusion | flops 1880621056 | bytes 7602180 | tf_op jit(solution)/shard_map/dot_general | solution.py:82
  259.9 3.1 fusion.33
  263.6 12.4 %collective-permute-done.10 = bf16[512,1024]{1,0:T(8,128)(2,1)S(1)} collective-permute-done((bf16[512,1024]{1,0:T(8,128)(2,1)S(1)}, bf16[512,1024]{1,0:T(8,128)(2,1)S(1)}, u32[]{:S(2)}, u32[]{:S(2)}) %collective-permute-start.10) | collective-permute-done | bytes 1048608 | tf_op jit(solution)/shard_map/ppermute | solution.py:24
  275.9 3.7 %collective-permute-done.16 = bf16[512,1024]{1,0:T(8,128)(2,1)S(1)} collective-permute-done((bf16[512,1024]{1,0:T(8,128)(2,1)S(1)}, bf16[512,1024]{1,0:T(8,128)(2,1)S(1)}, u32[]{:S(2)}, u32[]{:S(2)}) %collective-permute-start.16) | collective-permute-done | bytes 1048608 | tf_op jit(solution)/shard_map/ppermute | solution.py:20
  279.7 3.1 add_convert_fusion.2
  282.8 5.9 %fusion.30 = bf16[512,1024]{1,0:T(8,128)(2,1)} fusion(bf16[1792,1024]{0,1:T(8,128)(2,1)} %copy-done.15, bf16[1024,7168]{1,0:T(8,128)(2,1)} %param.5, s32[]{:T(128)S(6)} %select_n.219, s32[]{:T(128)S(6)} %select_n.217), kind=kOutput, calls=%fused_computation.45 | convolution fusion | flops 1879572480 | bytes 6553608 | tf_op jit(solution)/shard_map/dot_general | solution.py:80
  289.2 9.2 %collective-permute-done.5 = bf16[512,1024]{1,0:T(8,128)(2,1)S(1)} collective-permute-done((bf16[512,1024]{1,0:T(8,128)(2,1)}, bf16[512,1024]{1,0:T(8,128)(2,1)S(1)}, u32[]{:S(2)}, u32[]{:S(2)}) %collective-permute-start.5) | collective-permute-done | bytes 1048608 | tf_op jit(solution)/shard_map/ppermute | solution.py:24
  298.4 5.7 %collective-permute-done.17 = bf16[512,1024]{1,0:T(8,128)(2,1)S(1)} collective-permute-done((bf16[512,1024]{1,0:T(8,128)(2,1)}, bf16[512,1024]{1,0:T(8,128)(2,1)S(1)}, u32[]{:S(2)}, u32[]{:S(2)}) %collective-permute-start.17) | collective-permute-done | bytes 1048608 | tf_op jit(solution)/shard_map/ppermute | solution.py:20
  304.2 3.1 add_convert_fusion.1
  307.3 8.4 %copy.10 = f32[1,1792,1024]{2,1,0:T(8,128)} copy(f32[1,1792,1024]{1,2,0:T(8,128)} %get-tuple-element.10) | data formatting | bytes 14680064
  315.7 5.2 %all-gather.1 = f32[4,1,1792]{2,1,0:T(1,128)S(1)} all-gather(f32[1,1,1792]{2,1,0:T(1,128)S(1)} %reshape.19), channel_id=2, replica_groups=mesh['dp'=4,'row'=2,'col'=4] {'col'}, dimensions={0}, use_global_device_ids=true | all-gather | bytes 35840 | tf_op jit(solution)/shard_map/all_gather | solution.py:114
  321.5 4.9 %fusion.28 = f32[512,1024]{1,0:T(8,128)S(1)} fusion(bf16[1792,1024]{0,1:T(8,128)(2,1)} %copy-done.15, bf16[1024,7168]{1,0:T(8,128)(2,1)} %param.5, s32[]{:T(128)S(6)} %select_n.215, s32[]{:T(128)S(6)} %select_n.217), kind=kOutput, calls=%fused_computation.43 | convolution fusion | flops 1879048192 | bytes 7602184 | tf_op jit(solution)/shard_map/dot_general | solution.py:82
  (92 shorter events, 40.5 us)
Async XLA Ops:
  3.3 29.3 %collective-permute-start.19 = (bf16[512,1024]{1,0:T(8,128)(2,1)}, bf16[512,1024]{1,0:T(8,128)(2,1)S(1)}, u32[]{:S(2)}, u32[]{:S(2)}) collective-permute-start(bf16[512,1024]{1,0:T(8,128)(2,1)} %constant_dynamic-slice_fusion), channel_id=1, source_target_pairs={{0,8},{8,16},{16,24},{24,0},{1,9},{9,17},{17,25},{25,1},{2,10},{10... | collective-permute-start | bytes 3145736 | tf_op jit(solution)/shard_map/ppermute | solution.py:20
  11.0 41.4 %collective-permute-start.11 = (bf16[256,1792]{1,0:T(8,128)(2,1)S(1)}, bf16[256,1792]{1,0:T(8,128)(2,1)}, u32[]{:S(2)}, u32[]{:S(2)}) collective-permute-start(bf16[256,1792]{1,0:T(8,128)(2,1)S(1)} %get-tuple-element.13), channel_id=1, source_target_pairs={{0,8},{8,16},{16,24},{24,0},{1,9},{9,17},{17,25},{25,1},{2,10},{10... | collective-permute-start | bytes 2752520 | tf_op jit(solution)/shard_map/ppermute | solution.py:20
  32.6 79.4 %collective-permute-start.20 = (bf16[512,1024]{1,0:T(8,128)(2,1)S(1)}, bf16[512,1024]{1,0:T(8,128)(2,1)}, u32[]{:S(2)}, u32[]{:S(2)}) collective-permute-start(bf16[512,1024]{1,0:T(8,128)(2,1)S(1)} %collective-permute-done.19), channel_id=1, source_target_pairs={{0,4},{4,0},{1,5},{5,1},{2,6},{6,2},{3,7},{7,3},{8,12},{12,8},{9,1... | collective-permute-start | bytes 3145736 | tf_op jit(solution)/shard_map/ppermute | solution.py:24
  34.3 36.9 %collective-permute-start.1 = (bf16[256,1792]{1,0:T(8,128)(2,1)}, bf16[256,1792]{1,0:T(8,128)(2,1)}, u32[]{:S(2)}, u32[]{:S(2)}) collective-permute-start(bf16[256,1792]{1,0:T(8,128)(2,1)} %get-tuple-element.11), channel_id=1, source_target_pairs={{0,24},{8,0},{16,8},{24,16},{1,25},{9,1},{17,9},{25,17},{2,26},{10... | collective-permute-start | bytes 2752520 | tf_op jit(solution)/shard_map/ppermute | solution.py:20
  36.1 74.4 %collective-permute-start.6 = (bf16[256,1792]{1,0:T(8,128)(2,1)}, bf16[256,1792]{1,0:T(8,128)(2,1)}, u32[]{:S(2)}, u32[]{:S(2)}) collective-permute-start(bf16[256,1792]{1,0:T(8,128)(2,1)} %get-tuple-element.12), channel_id=1, source_target_pairs={{0,16},{8,24},{16,0},{24,8},{1,17},{9,25},{17,1},{25,9},{2,18},{10... | collective-permute-start | bytes 2752520 | tf_op jit(solution)/shard_map/ppermute | solution.py:20
  52.4 59.6 %collective-permute-start.12 = (bf16[256,1792]{1,0:T(8,128)(2,1)}, bf16[256,1792]{1,0:T(8,128)(2,1)}, u32[]{:S(2)}, u32[]{:S(2)}) collective-permute-start(bf16[256,1792]{1,0:T(8,128)(2,1)} %collective-permute-done.11), channel_id=1, source_target_pairs={{0,2},{1,3},{2,0},{3,1},{4,6},{5,7},{6,4},{7,5},{8,10},{9,11},{10,... | collective-permute-start | bytes 2752520 | tf_op jit(solution)/shard_map/ppermute | solution.py:24
  63.3 58.9 %collective-permute-start.14 = (bf16[256,1792]{1,0:T(8,128)(2,1)}, bf16[256,1792]{1,0:T(8,128)(2,1)S(1)}, u32[]{:S(2)}, u32[]{:S(2)}) collective-permute-start(bf16[256,1792]{1,0:T(8,128)(2,1)} %collective-permute-done.11), channel_id=1, source_target_pairs={{0,1},{1,0},{2,3},{3,2},{4,5},{5,4},{6,7},{7,6},{8,9},{9,8},{10,11... | collective-permute-start | bytes 2752520 | tf_op jit(solution)/shard_map/ppermute | solution.py:24
  71.2 50.4 %collective-permute-start.2 = (bf16[256,1792]{1,0:T(8,128)(2,1)}, bf16[256,1792]{1,0:T(8,128)(2,1)S(1)}, u32[]{:S(2)}, u32[]{:S(2)}) collective-permute-start(bf16[256,1792]{1,0:T(8,128)(2,1)} %collective-permute-done.1), channel_id=1, source_target_pairs={{0,2},{1,3},{2,0},{3,1},{4,6},{5,7},{6,4},{7,5},{8,10},{9,11},{10,... | collective-permute-start | bytes 2752520 | tf_op jit(solution)/shard_map/ppermute | solution.py:24
  110.5 22.4 %collective-permute-start.7 = (bf16[256,1792]{1,0:T(8,128)(2,1)}, bf16[256,1792]{1,0:T(8,128)(2,1)S(1)}, u32[]{:S(2)}, u32[]{:S(2)}) collective-permute-start(bf16[256,1792]{1,0:T(8,128)(2,1)} %collective-permute-done.6), channel_id=1, source_target_pairs={{0,2},{1,3},{2,0},{3,1},{4,6},{5,7},{6,4},{7,5},{8,10},{9,11},{10,... | collective-permute-start | bytes 2752520 | tf_op jit(solution)/shard_map/ppermute | solution.py:24
  112.0 26.6 %collective-permute-start.21 = (bf16[512,1024]{1,0:T(8,128)(2,1)S(1)}, bf16[512,1024]{1,0:T(8,128)(2,1)S(1)}, u32[]{:S(2)}, u32[]{:S(2)}) collective-permute-start(bf16[512,1024]{1,0:T(8,128)(2,1)S(1)} %collective-permute-done.19), channel_id=1, source_target_pairs={{0,8},{8,16},{16,24},{24,0},{1,9},{9,17},{17,25},{25,1},{2,10},{10... | collective-permute-start | bytes 3145736 | tf_op jit(solution)/shard_map/ppermute | solution.py:20
  112.0 26.6 %collective-permute-start.13 = (bf16[256,1792]{1,0:T(8,128)(2,1)}, bf16[256,1792]{1,0:T(8,128)(2,1)S(1)}, u32[]{:S(2)}, u32[]{:S(2)}) collective-permute-start(bf16[256,1792]{1,0:T(8,128)(2,1)} %collective-permute-done.12), channel_id=1, source_target_pairs={{0,1},{1,0},{2,3},{3,2},{4,5},{5,4},{6,7},{7,6},{8,9},{9,8},{10,11... | collective-permute-start | bytes 2752520 | tf_op jit(solution)/shard_map/ppermute | solution.py:24
  121.6 27.0 %collective-permute-start.4 = (bf16[256,1792]{1,0:T(8,128)(2,1)}, bf16[256,1792]{1,0:T(8,128)(2,1)S(1)}, u32[]{:S(2)}, u32[]{:S(2)}) collective-permute-start(bf16[256,1792]{1,0:T(8,128)(2,1)} %collective-permute-done.1), channel_id=1, source_target_pairs={{0,1},{1,0},{2,3},{3,2},{4,5},{5,4},{6,7},{7,6},{8,9},{9,8},{10,11... | collective-permute-start | bytes 2752520 | tf_op jit(solution)/shard_map/ppermute | solution.py:24
  122.2 35.7 %collective-permute-start.9 = (bf16[256,1792]{1,0:T(8,128)(2,1)}, bf16[256,1792]{1,0:T(8,128)(2,1)S(1)}, u32[]{:S(2)}, u32[]{:S(2)}) collective-permute-start(bf16[256,1792]{1,0:T(8,128)(2,1)} %collective-permute-done.6), channel_id=1, source_target_pairs={{0,1},{1,0},{2,3},{3,2},{4,5},{5,4},{6,7},{7,6},{8,9},{9,8},{10,11... | collective-permute-start | bytes 2752520 | tf_op jit(solution)/shard_map/ppermute | solution.py:24
  132.9 21.7 %collective-permute-start.3 = (bf16[256,1792]{1,0:T(8,128)(2,1)S(1)}, bf16[256,1792]{1,0:T(8,128)(2,1)S(1)}, u32[]{:S(2)}, u32[]{:S(2)}) collective-permute-start(bf16[256,1792]{1,0:T(8,128)(2,1)S(1)} %collective-permute-done.2), channel_id=1, source_target_pairs={{0,1},{1,0},{2,3},{3,2},{4,5},{5,4},{6,7},{7,6},{8,9},{9,8},{10,11... | collective-permute-start | bytes 2752520 | tf_op jit(solution)/shard_map/ppermute | solution.py:24
  138.5 19.4 %collective-permute-start.8 = (bf16[256,1792]{1,0:T(8,128)(2,1)S(1)}, bf16[256,1792]{1,0:T(8,128)(2,1)S(1)}, u32[]{:S(2)}, u32[]{:S(2)}) collective-permute-start(bf16[256,1792]{1,0:T(8,128)(2,1)S(1)} %collective-permute-done.7), channel_id=1, source_target_pairs={{0,1},{1,0},{2,3},{3,2},{4,5},{5,4},{6,7},{7,6},{8,9},{9,8},{10,11... | collective-permute-start | bytes 2752520 | tf_op jit(solution)/shard_map/ppermute | solution.py:24
  138.5 41.0 %collective-permute-start.22 = (bf16[512,1024]{1,0:T(8,128)(2,1)S(1)}, bf16[512,1024]{1,0:T(8,128)(2,1)S(1)}, u32[]{:S(2)}, u32[]{:S(2)}) collective-permute-start(bf16[512,1024]{1,0:T(8,128)(2,1)S(1)} %collective-permute-done.21), channel_id=1, source_target_pairs={{0,4},{4,0},{1,5},{5,1},{2,6},{6,2},{3,7},{7,3},{8,12},{12,8},{9,1... | collective-permute-start | bytes 3145736 | tf_op jit(solution)/shard_map/ppermute | solution.py:24
  148.6 28.3 %collective-permute-start.23 = (bf16[512,1024]{1,0:T(8,128)(2,1)S(1)}, bf16[512,1024]{1,0:T(8,128)(2,1)S(1)}, u32[]{:S(2)}, u32[]{:S(2)}) collective-permute-start(bf16[512,1024]{1,0:T(8,128)(2,1)S(1)} %collective-permute-done.21), channel_id=1, source_target_pairs={{0,8},{8,16},{16,24},{24,0},{1,9},{9,17},{17,25},{25,1},{2,10},{10... | collective-permute-start | bytes 3145736 | tf_op jit(solution)/shard_map/ppermute | solution.py:20
  159.4 20.3 %copy-start.9 = (bf16[256,1792]{1,0:T(8,128)(2,1)}, bf16[256,1792]{1,0:T(8,128)(2,1)S(1)}, u32[]{:S(2)}) copy-start(bf16[256,1792]{1,0:T(8,128)(2,1)S(1)} %get-tuple-element.19) | copy-start | bytes 2752516
  177.0 24.0 %collective-permute-start.24 = (bf16[512,1024]{1,0:T(8,128)(2,1)S(1)}, bf16[512,1024]{1,0:T(8,128)(2,1)S(1)}, u32[]{:S(2)}, u32[]{:S(2)}) collective-permute-start(bf16[512,1024]{1,0:T(8,128)(2,1)S(1)} %collective-permute-done.23), channel_id=1, source_target_pairs={{0,4},{4,0},{1,5},{5,1},{2,6},{6,2},{3,7},{7,3},{8,12},{12,8},{9,1... | collective-permute-start | bytes 3145736 | tf_op jit(solution)/shard_map/ppermute | solution.py:24
  227.2 26.4 %collective-permute-start.15 = (bf16[512,1024]{1,0:T(8,128)(2,1)}, bf16[512,1024]{1,0:T(8,128)(2,1)}, u32[]{:S(2)}, u32[]{:S(2)}) collective-permute-start(bf16[512,1024]{1,0:T(8,128)(2,1)} %fusion.39), channel_id=1, source_target_pairs={{0,4},{4,0},{1,5},{5,1},{2,6},{6,2},{3,7},{7,3},{8,12},{12,8},{9,1... | collective-permute-start | bytes 3145736 | tf_op jit(solution)/shard_map/ppermute | solution.py:24
  232.9 20.7 %copy-start.3 = (bf16[1024,1792]{1,0:T(8,128)(2,1)S(1)}, bf16[1024,1792]{1,0:T(8,128)(2,1)}, u32[]{:S(2)}) copy-start(bf16[1024,1792]{1,0:T(8,128)(2,1)} %pad_maximum_fusion.2) | copy-start | bytes 11010052
  235.0 24.6 %copy-start.6 = (bf16[256,1792]{1,0:T(8,128)(2,1)S(1)}, bf16[256,1792]{1,0:T(8,128)(2,1)}, u32[]{:S(2)}) copy-start(bf16[256,1792]{1,0:T(8,128)(2,1)} %get-tuple-element.16) | copy-start | bytes 2752516
  235.0 24.5 %copy-start.7 = (bf16[256,1792]{1,0:T(8,128)(2,1)S(1)}, bf16[256,1792]{1,0:T(8,128)(2,1)}, u32[]{:S(2)}) copy-start(bf16[256,1792]{1,0:T(8,128)(2,1)} %get-tuple-element.17) | copy-start | bytes 2752516
  235.0 24.5 %copy-start.8 = (bf16[256,1792]{1,0:T(8,128)(2,1)S(1)}, bf16[256,1792]{1,0:T(8,128)(2,1)}, u32[]{:S(2)}) copy-start(bf16[256,1792]{1,0:T(8,128)(2,1)} %get-tuple-element.18) | copy-start | bytes 2752516
  235.0 40.9 %collective-permute-start.10 = (bf16[512,1024]{1,0:T(8,128)(2,1)S(1)}, bf16[512,1024]{1,0:T(8,128)(2,1)S(1)}, u32[]{:S(2)}, u32[]{:S(2)}) collective-permute-start(bf16[512,1024]{1,0:T(8,128)(2,1)S(1)} %fusion.36), channel_id=1, source_target_pairs={{0,4},{4,0},{1,5},{5,1},{2,6},{6,2},{3,7},{7,3},{8,12},{12,8},{9,1... | collective-permute-start | bytes 3145736 | tf_op jit(solution)/shard_map/ppermute | solution.py:24
  256.9 22.8 %collective-permute-start.16 = (bf16[512,1024]{1,0:T(8,128)(2,1)S(1)}, bf16[512,1024]{1,0:T(8,128)(2,1)S(1)}, u32[]{:S(2)}, u32[]{:S(2)}) collective-permute-start(bf16[512,1024]{1,0:T(8,128)(2,1)S(1)} %add_convert_fusion.3), channel_id=1, source_target_pairs={{0,8},{8,16},{16,24},{24,0},{1,9},{9,17},{17,25},{25,1},{2,10},{10... | collective-permute-start | bytes 3145736 | tf_op jit(solution)/shard_map/ppermute | solution.py:20
  263.1 35.4 %collective-permute-start.5 = (bf16[512,1024]{1,0:T(8,128)(2,1)}, bf16[512,1024]{1,0:T(8,128)(2,1)S(1)}, u32[]{:S(2)}, u32[]{:S(2)}) collective-permute-start(bf16[512,1024]{1,0:T(8,128)(2,1)} %fusion.33), channel_id=1, source_target_pairs={{0,4},{4,0},{1,5},{5,1},{2,6},{6,2},{3,7},{7,3},{8,12},{12,8},{9,1... | collective-permute-start | bytes 3145736 | tf_op jit(solution)/shard_map/ppermute | solution.py:24
  282.8 21.4 %collective-permute-start.17 = (bf16[512,1024]{1,0:T(8,128)(2,1)}, bf16[512,1024]{1,0:T(8,128)(2,1)S(1)}, u32[]{:S(2)}, u32[]{:S(2)}) collective-permute-start(bf16[512,1024]{1,0:T(8,128)(2,1)} %add_convert_fusion.2), channel_id=1, source_target_pairs={{0,8},{8,16},{16,24},{24,0},{1,9},{9,17},{17,25},{25,1},{2,10},{10... | collective-permute-start | bytes 3145736 | tf_op jit(solution)/shard_map/ppermute | solution.py:20
  282.8 21.4 %copy-start.5 = (bf16[1024,1792]{1,0:T(8,128)(2,1)S(1)}, bf16[1024,1792]{1,0:T(8,128)(2,1)}, u32[]{:S(2)}) copy-start(bf16[1024,1792]{1,0:T(8,128)(2,1)} %copy-done.4) | copy-start | bytes 11010052
  282.8 21.4 %copy-start.17 = (bf16[1792,1024]{0,1:T(8,128)(2,1)S(1)}, bf16[1792,1024]{0,1:T(8,128)(2,1)}, u32[]{:S(2)}) copy-start(bf16[1792,1024]{0,1:T(8,128)(2,1)} %copy-done.15) | copy-start | bytes 11010052
  288.7 37.8 %collective-permute-start = (bf16[512,1024]{1,0:T(8,128)(2,1)}, bf16[512,1024]{1,0:T(8,128)(2,1)S(1)}, u32[]{:S(2)}, u32[]{:S(2)}) collective-permute-start(bf16[512,1024]{1,0:T(8,128)(2,1)} %fusion.30), channel_id=1, source_target_pairs={{0,4},{4,0},{1,5},{5,1},{2,6},{6,2},{3,7},{7,3},{8,12},{12,8},{9,1... | collective-permute-start | bytes 3145736 | tf_op jit(solution)/shard_map/ppermute | solution.py:24
  307.3 20.6 %collective-permute-start.18 = (bf16[512,1024]{1,0:T(8,128)(2,1)}, bf16[512,1024]{1,0:T(8,128)(2,1)}, u32[]{:S(2)}, u32[]{:S(2)}) collective-permute-start(bf16[512,1024]{1,0:T(8,128)(2,1)} %add_convert_fusion.1), channel_id=1, source_target_pairs={{0,8},{8,16},{16,24},{24,0},{1,9},{9,17},{17,25},{25,1},{2,10},{10... | collective-permute-start | bytes 3145736 | tf_op jit(solution)/shard_map/ppermute | solution.py:20
  (13 other events, 127.1 us)
